TPU v7x, 512 devices: a whole 4x8x8 slice. The times are simulated.
512 devices in a mesh: tm: 8 (over x, core), src: 64 (over y, z).
Axes of the slice: x: 4, y: 8, z: 8, core: 2. Of those that a mesh axis runs over, the one named last changes fastest.
Arguments:
- design: float32 [16, 8388608], P(None, ('tm', 'src')), may hold values from -2 to 2
- unit_index: int32 [8388608], P(('tm', 'src')), may hold values from 0 to 4095, as said below
- residual: float32 [8388608], P(('tm', 'src')), may hold values from -6 to 6
- weight: float32 [8388608], P(('tm', 'src')), may hold values from 0.25 to 4
- obs_count: int32 [512], P(('tm', 'src')), may hold values from 1 to 16384, as said below
- damping: float32 [4096], P(('tm', 'src')), may hold values from 1 to 10
Outputs:
- solution: float32 [16, 4096], P(None, ('tm', 'src'))
- misfit: float32 [], replicated
Inputs may be any that keep to these rules, and one draw needn't show every extreme that they name: `unit_index`: an observation on a device of tm index g names a unit in [g * 512, (g + 1) * 512). `obs_count`: some device has all 16384 slots live.
All inputs are finite; a program needn't handle non-finite values.
Results may differ from a plain program's by a relative error of at most 0.0003.
Values sent between devices are 32-bit elements; how exact they have to be, the bound alone decides.
A program may use at most 64 MiB of HBM per device.

v0:
```python
import jax
import jax.numpy as jnp
from jax import lax
from jax.sharding import Mesh
from jax.sharding import PartitionSpec as P

SRC = ("src_0", "src_1")
TM = ("tm_0", "tm_1")
TM_SRC = ("tm_0", "tm_1", "src_0", "src_1")


def in_blocks(x, dim, devices):
    dims = x.shape
    pieces = x.reshape(*dims[:dim], devices, dims[dim] // devices, *dims[dim + 1 :])
    return jnp.moveaxis(pieces, dim, 0)


def summed_on_arrival(x, axis, dim):
    pieces = in_blocks(x, dim, lax.axis_size(axis))
    arrived = lax.all_to_all(pieces, axis, split_axis=0, concat_axis=0, tiled=True)
    return arrived.sum(axis=0)


def by_axis(x, axes):
    for axis in axes:
        x = lax.psum(x, axis)
    return x


def make_reader(stacked):

    def reader(row, column):
        return stacked[row * 16 + column]

    return reader


def block_solve(reader, rhs, damping):
    lower = {}
    for j in range(16):
        running = reader(j, j) + damping
        for k in range(j):
            running = running - lower[j, k] * lower[j, k]
        diag_term = jnp.sqrt(running)
        lower[j, j] = diag_term
        for i in range(j + 1, 16):
            running = reader(i, j)
            for k in range(j):
                running = running - lower[i, k] * lower[j, k]
            lower[i, j] = running / diag_term
    forward = []
    for i in range(16):
        running = rhs[i]
        for k in range(i):
            running = running - lower[i, k] * forward[k]
        forward.append(running / lower[i, i])
    backward = [None] * 16
    for i in range(15, -1, -1):
        running = forward[i]
        for k in range(i + 1, 16):
            running = running - lower[k, i] * backward[k]
        backward[i] = running / lower[i, i]
    return jnp.stack(backward)


def quadratic_terms(reader, rhs, solution_own):
    quadratic = jnp.zeros((), jnp.float32)
    for i in range(16):
        applied = jnp.zeros_like(solution_own[0])
        for j in range(16):
            applied = applied + reader(max(i, j), min(i, j)) * solution_own[j]
        quadratic = quadratic + jnp.sum(solution_own[i] * applied)
    return quadratic - 2.0 * jnp.sum(solution_own * rhs)


def on_device(design, unit_index, residual, weight, obs_count, damping):
    n_source = lax.axis_size(SRC)
    own_units = damping.shape[0]
    units_group = own_units * n_source
    slots = design.shape[1]
    local_unit = unit_index - lax.axis_index(TM) * units_group
    weights_on = jnp.where(
        jnp.arange(slots, dtype=jnp.int32) < obs_count[0], weight, jnp.zeros_like(weight)
    )
    block_rows = 1024
    turns = slots // block_rows
    pair_count = 256

    def pair_rows(rows):
        return (rows[:, None, :] * rows[None, :, :]).reshape(256, rows.shape[1])

    unit_range = jnp.arange(units_group, dtype=jnp.int32)

    def accumulate(step, partial_value):
        begin = step * block_rows
        rows = lax.dynamic_slice_in_dim(design, begin, block_rows, 1)
        units_of = lax.dynamic_slice_in_dim(local_unit, begin, block_rows, 0)
        resid = lax.dynamic_slice_in_dim(residual, begin, block_rows, 0)
        weights_blk = lax.dynamic_slice_in_dim(weights_on, begin, block_rows, 0)
        stacked = jnp.concatenate(
            [pair_rows(rows) * weights_blk, rows * (weights_blk * resid)], axis=0
        )
        one_hot = (units_of[:, None] == unit_range[None, :]).astype(jnp.float32)
        return partial_value + jnp.dot(
            stacked, one_hot, precision=lax.Precision.HIGHEST, preferred_element_type=jnp.float32
        )

    start = jnp.zeros((pair_count + 16, units_group), jnp.float32)
    partial_value = lax.fori_loop(0, turns, accumulate, start)
    own_part = summed_on_arrival(partial_value, SRC, 1)
    solution_own = block_solve(make_reader(own_part), own_part[pair_count:], damping)
    unit_terms = quadratic_terms(make_reader(own_part), own_part[pair_count:], solution_own)
    before = jnp.sum(weights_on * residual * residual)
    chi_total, weight_total = (
        by_axis(before + unit_terms, TM_SRC),
        by_axis(jnp.sum(weights_on), TM_SRC),
    )
    return (solution_own, chi_total / weight_total)


def solution(mesh):
    torus = Mesh(mesh.devices.reshape(4, 2, 8, 8), ("tm_0", "tm_1", "src_0", "src_1"))
    return jax.shard_map(
        on_device,
        mesh=torus,
        in_specs=(P(None, TM_SRC), P(TM_SRC), P(TM_SRC), P(TM_SRC), P(TM_SRC), P(TM_SRC)),
        out_specs=(P(None, TM_SRC), P()),
        check_vma=False,
    )
```

profile of v0, /device:TPU:8, one launch (start us, length us, event | category | flops | bytes accessed | tf_op | source)
XLA Modules:
  0.0 174.0 jit_solution(1141471634184720458)
XLA Ops:
  2.1 1.6 fusion.12
  3.7 52.6 %while.14 = (s32[]{:T(128)}, f32[272,512]{1,0:T(8,128)S(1)}, f32[16,16384]{1,0:T(8,128)}, f32[16384]{0:T(1024)S(1)}, f32[16384]{0:T(1024)}, /*index=5*/s32[16384...) while((s32[]{:T(128)}, f32[272,512]{1,0:T(8,128)S(1)}, f32[16,16384]{1,0:T(8,128)}, ...), condition=%wide.region_1.2_spmd.clone, body=%wide.region_0.1_spmd.clone.sunk | while | flops 1712899072 | bytes 5673129 | solution.py:109
  5.5 1.4 fusion.17
  8.8 1.4 fusion.17
  12.1 1.4 fusion.17
  15.4 1.4 fusion.17
  18.7 1.4 fusion.17
  22.0 1.4 fusion.17
  25.3 1.4 fusion.17
  28.6 1.4 fusion.17
  31.8 1.4 fusion.17
  35.1 1.4 fusion.17
  38.4 1.4 fusion.17
  41.7 1.4 fusion.17
  45.0 1.4 fusion.17
  48.3 1.4 fusion.17
  51.6 1.4 fusion.17
  54.9 1.4 fusion.17
  56.6 40.2 %all_to_all.5 = f32[64,272,8]{1,2,0:T(8,128)S(1)} all-to-all(f32[64,272,8]{1,2,0:T(8,128)S(1)} %bitcast.25), channel_id=1, replica_groups=mesh['tm_0'=4,'tm_1'=2,'src_0'=8,'src_1'=8] {'src_0','src_1'}, dimensions={0} | all-to-all | bytes 1114112 | tf_op jit(solution)/shard_map/all_to_all | solution.py:20
  101.6 0.9 multiply_reduce_fusion
  125.5 11.0 %all-reduce.2 = (f32[]{:T(128)}, f32[]{:T(128)}) all-reduce(f32[]{:T(128)S(6)} %add.1140, f32[]{:T(128)} %get-tuple-element.154), channel_id=1, replica_groups=mesh['tm_0'=4,'tm_1'=2,'src_0'=8,'src_1'=8] {'tm_0'}, use_global_device_ids=true, to_apply=%region_21.22 | all-reduce | flops 2 | bytes 16 | tf_op jit(solution)/shard_map/psum | solution.py:26
  136.5 3.2 %all-reduce.3 = (f32[]{:T(128)}, f32[]{:T(128)}) all-reduce(f32[]{:T(128)} %get-tuple-element.324, f32[]{:T(128)} %get-tuple-element.325), channel_id=1, replica_groups=mesh['tm_0'=4,'tm_1'=2,'src_0'=8,'src_1'=8] {'tm_1'}, use_global_device_ids=true, to_apply=%region_22.23 | all-reduce | flops 2 | bytes 16 | tf_op jit(solution)/shard_map/psum | solution.py:26
  139.7 16.0 %all-reduce.1 = (f32[]{:T(128)}, f32[]{:T(128)}) all-reduce(f32[]{:T(128)} %get-tuple-element.326, f32[]{:T(128)} %get-tuple-element.327), channel_id=1, replica_groups=mesh['tm_0'=4,'tm_1'=2,'src_0'=8,'src_1'=8] {'src_0'}, use_global_device_ids=true, to_apply=%region_23.24 | all-reduce | flops 2 | bytes 16 | tf_op jit(solution)/shard_map/psum | solution.py:26
  155.7 15.8 %all-reduce = (f32[]{:T(128)}, f32[]{:T(128)}) all-reduce(f32[]{:T(128)} %get-tuple-element.322, f32[]{:T(128)} %get-tuple-element.323), channel_id=1, replica_groups=mesh['tm_0'=4,'tm_1'=2,'src_0'=8,'src_1'=8] {'src_1'}, use_global_device_ids=true, to_apply=%region_24.25 | all-reduce | flops 2 | bytes 16 | tf_op jit(solution)/shard_map/psum | solution.py:26
  (131 shorter events, 46.5 us)
Async XLA Ops:
  96.8 4.2 %copy-start.1 = (f32[8]{0:T(128)S(1)}, f32[8]{0:T(128)}, u32[]{:S(2)}) copy-start(f32[8]{0:T(128)} %param.13) | copy-start | bytes 100
  113.8 59.1 %copy-start = (f32[16,8]{0,1:T(8,128)}, f32[16,8]{0,1:T(8,128)S(1)}, u32[]{:S(2)}) copy-start(f32[16,8]{0,1:T(8,128)S(1)} %stack.67) | copy-start | bytes 1540
where the time goes:
time: 176 us; the launch traced here: 174 us
  blocking collectives  86.2 us (49%)
  other arithmetic  43.1 us (24%)
  matrix products  22.9 us (13%)
  between operations  15 us (9%)
  local copies, waits for them, and re-layouts  5.88 us (3%)
    psum x4, blocking collectives, by_axis(): x = lax.psum(x, axis)  46 us
    all_to_all x1, blocking collectives, summed_on_arrival(): lax.all_to_all(pieces, axis, split_axis=0, concat_axis=0, tiled=True)  40.2 us
    dot_general x16, matrix products, accumulate(): jnp.dot(stacked, one_hot, precision=lax.Precision.HIGHEST, preferred_elem...  22.9 us
    mul x16, other arithmetic, accumulate(): rows * (weights_blk * resid)  13.6 us
    mul x16, other arithmetic, accumulate(): weights_blk * resid  11.1 us
    reduce_sum x16, other arithmetic, quadratic_terms(): quadratic = quadratic + jnp.sum(solution_own[i] * applied)  10.8 us
    slice x7, local copies, waits for them, and re-layouts, block_solve(): running = rhs[i]  3.55 us

commit v1 on v0

--- a/solution.py
+++ b/solution.py
@@ -7,6 +7,10 @@
 SRC = ("src_0", "src_1")
 TM = ("tm_0", "tm_1")
 TM_SRC = ("tm_0", "tm_1", "src_0", "src_1")
+
+
+def _serve_sites(peer_axis, array_here):
+    return jnp.sum(lax.all_gather(array_here, peer_axis), axis=0)
 
 
 def in_blocks(x, dim, devices):
@@ -23,7 +27,7 @@
 
 def by_axis(x, axes):
     for axis in axes:
-        x = lax.psum(x, axis)
+        x = _serve_sites(axis, x)
     return x
 
 

time: 176 us -> 193 us (1.097)
  blocking collectives: 86.2 us -> 43.3 us
  waiting for transfers between devices: 0 us -> 21.3 us
  starting transfers between devices: 0 us -> 16.6 us
  local copies, waits for them, and re-layouts: 5.88 us -> 22.4 us
  other arithmetic: 43.1 us -> 47.9 us
    psum x4 -> x0, blocking collectives: 46 us -> none  [by_axis(): x = lax.psum(x, axis)]
    unnamed x0 -> x4, blocking collectives: none -> 43.3 us
    all_to_all x1 -> x0, blocking collectives: 40.2 us -> none  [summed_on_arrival(): lax.all_to_all(pieces, axis, split_axis=0, concat_axis=0, tiled=True)]
    all_to_all x0 -> x1, waiting for transfers between devices: none -> 21.3 us  [summed_on_arrival(): lax.all_to_all(pieces, axis, split_axis=0, concat_axis=0, tiled=True)]
    all_to_all x0 -> x1, starting transfers between devices: none -> 16.6 us  [summed_on_arrival(): lax.all_to_all(pieces, axis, split_axis=0, concat_axis=0, tiled=True)]
    unnamed x4 -> x24, local copies, waits for them, and re-layouts: 0.01 us -> 15.6 us
    reduce_sum x0 -> x8, other arithmetic: none -> 4.87 us  [_serve_sites(): return jnp.sum(lax.all_gather(array_here, peer_axis), axis=0)]
  transfers between devices with their start and end apart: 0 -> 1, of which waited for: 0 -> 1; matrix products, arithmetic and copies ran while one was open for 0% -> 1% of each run, Pallas kernels for 0% -> 0%
where the time goes in v1:
time: 193 us; the launch traced here: 191 us
  other arithmetic  47.9 us (25%)
  blocking collectives  43.3 us (22%)
  matrix products  22.9 us (12%)
  local copies, waits for them, and re-layouts  22.4 us (12%)
  waiting for transfers between devices  21.3 us (11%)
  starting transfers between devices  16.6 us (9%)
  between operations  15.1 us (8%)
    unnamed x4, blocking collectives  43.3 us
    dot_general x16, matrix products, accumulate(): jnp.dot(stacked, one_hot, precision=lax.Precision.HIGHEST, preferred_elem...  22.9 us
    all_to_all x1, waiting for transfers between devices, summed_on_arrival(): lax.all_to_all(pieces, axis, split_axis=0, concat_axis=0, tiled=True)  21.3 us
    all_to_all x1, starting transfers between devices, summed_on_arrival(): lax.all_to_all(pieces, axis, split_axis=0, concat_axis=0, tiled=True)  16.6 us
    unnamed x24, local copies, waits for them, and re-layouts  15.6 us
    mul x16, other arithmetic, accumulate(): rows * (weights_blk * resid)  13.6 us
    mul x16, other arithmetic, accumulate(): weights_blk * resid  11.1 us
    reduce_sum x16, other arithmetic, quadratic_terms(): quadratic = quadratic + jnp.sum(solution_own[i] * applied)  10.7 us
  transfers between devices with their start and end apart: 1, of which 1 were waited for; matrix products, arithmetic and copies ran while one was open for 1% of the time, Pallas kernels for 0%

profile of v1, /device:TPU:8, one launch (start us, length us, event | category | flops | bytes accessed | tf_op | source)
XLA Modules:
  0.0 190.5 jit_solution(13602585734821873553)
XLA Ops:
  2.1 1.6 fusion.12
  3.7 52.6 %while.14 = (s32[]{:T(128)}, f32[272,512]{1,0:T(8,128)S(1)}, f32[16,16384]{1,0:T(8,128)}, f32[16384]{0:T(1024)S(1)}, f32[16384]{0:T(1024)}, /*index=5*/s32[16384...) while((s32[]{:T(128)}, f32[272,512]{1,0:T(8,128)S(1)}, f32[16,16384]{1,0:T(8,128)}, ...), condition=%wide.region_1.2_spmd.clone, body=%wide.region_0.1_spmd.clone.sunk | while | flops 1712899072 | bytes 5673129 | solution.py:113
  5.5 1.4 fusion.17
  12.1 1.4 fusion.17
  15.4 1.4 fusion.17
  18.7 1.4 fusion.17
  22.0 1.4 fusion.17
  28.5 1.4 fusion.17
  31.8 1.4 fusion.17
  35.1 1.4 fusion.17
  38.4 1.4 fusion.17
  45.0 1.4 fusion.17
  48.3 1.4 fusion.17
  51.6 1.4 fusion.17
  54.8 1.4 fusion.17
  57.4 16.6 %all-to-all-start = ((f32[64,272,8]{1,2,0:T(8,128)}), f32[64,272,8]{1,2,0:T(8,128)S(1)}, u32[]{:S(2)}, u32[]{:S(2)}) async-start(f32[64,272,8]{1,2,0:T(8,128)} %bitcast.2), calls=%async_computation | async-start | bytes 1572864 | tf_op jit(solution)/shard_map/all_to_all | solution.py:24
  76.6 21.3 %all-to-all-done = f32[64,272,8]{1,2,0:T(8,128)S(1)} async-done(((f32[64,272,8]{1,2,0:T(8,128)}), f32[64,272,8]{1,2,0:T(8,128)S(1)}, u32[]{:S(2)}, u32[]{:S(2)}) %all-to-all-start) | async-done | bytes 557088 | tf_op jit(solution)/shard_map/all_to_all | solution.py:24
  128.7 10.5 %all-reduce.10 = (f32[4]{0:T(128)S(1)}, f32[4]{0:T(128)S(1)}) all-reduce(f32[4]{0:T(128)S(1)} %dynamic-update-slice, f32[4]{0:T(128)S(1)} %dynamic-update-slice.4), channel_id=1, replica_groups=mesh['tm_0'=4,'tm_1'=2,'src_0'=8,'src_1'=8] {'tm_0'}, use_global_device_ids=true, to_apply=%add | all-reduce | flops 8 | bytes 64
  141.7 1.4 dynamic-update-slice.1
  144.5 2.4 %all-reduce.11 = (f32[2]{0:T(128)S(1)}, f32[2]{0:T(128)S(1)}) all-reduce(f32[2]{0:T(128)S(1)} %dynamic-update-slice.1, f32[2]{0:T(128)S(1)} %dynamic-update-slice.5), channel_id=1, replica_groups=mesh['tm_0'=4,'tm_1'=2,'src_0'=8,'src_1'=8] {'tm_1'}, use_global_device_ids=true, to_apply=%add.1 | all-reduce | flops 4 | bytes 32
  149.5 1.4 dynamic-update-slice.2
  152.3 15.4 %all-reduce.9 = (f32[8]{0:T(128)S(1)}, f32[8]{0:T(128)S(1)}) all-reduce(f32[8]{0:T(128)S(1)} %dynamic-update-slice.2, f32[8]{0:T(128)S(1)} %dynamic-update-slice.6), channel_id=1, replica_groups=mesh['tm_0'=4,'tm_1'=2,'src_0'=8,'src_1'=8] {'src_0'}, use_global_device_ids=true, to_apply=%add.2 | all-reduce | flops 16 | bytes 128
  170.2 1.4 dynamic-update-slice.3
  171.7 15.1 %all-reduce.8 = (f32[8]{0:T(128)S(1)}, f32[8]{0:T(128)S(1)}) all-reduce(f32[8]{0:T(128)S(1)} %dynamic-update-slice.3, f32[8]{0:T(128)S(1)} %dynamic-update-slice.7), channel_id=1, replica_groups=mesh['tm_0'=4,'tm_1'=2,'src_0'=8,'src_1'=8] {'src_1'}, use_global_device_ids=true, to_apply=%add.3 | all-reduce | flops 16 | bytes 128
  (160 shorter events, 68.7 us)
Async XLA Ops:
  57.4 40.4 %all-to-all-start = ((f32[64,272,8]{1,2,0:T(8,128)}), f32[64,272,8]{1,2,0:T(8,128)S(1)}, u32[]{:S(2)}, u32[]{:S(2)}) async-start(f32[64,272,8]{1,2,0:T(8,128)} %bitcast.2), calls=%async_computation | async-start | bytes 1572864 | tf_op jit(solution)/shard_map/all_to_all | solution.py:24
  74.0 28.0 %copy-start.1 = (f32[8]{0:T(128)S(1)}, f32[8]{0:T(128)}, u32[]{:S(2)}) copy-start(f32[8]{0:T(128)} %param.13) | copy-start | bytes 100
  114.8 74.6 %copy-start = (f32[16,8]{0,1:T(8,128)}, f32[16,8]{0,1:T(8,128)S(1)}, u32[]{:S(2)}) copy-start(f32[16,8]{0,1:T(8,128)S(1)} %stack.67) | copy-start | bytes 1540
